TPU v7x, 32 devices: a whole 2x2x4 slice. The times are simulated.
32 devices in a mesh: row: 8 (over z, y), col: 4 (over x, core).
Axes of the slice: x: 2, y: 2, z: 4, core: 2. Of those that a mesh axis runs over, the one named last changes fastest.
Arguments:
- tile_seeds: int32 [32, 8, 64, 4], P(None, 'row', None, 'col'), may hold values from 0 to 1073741823
- factors: bfloat16 [32, 1024, 64, 512], P(None, 'row', None, 'col'), may hold values from -0.015625 to 0.015625
- lower_inverse: bfloat16 [4, 16, 512, 8, 1024], P(None, None, 'col', None, 'row'), may hold values from -0.1 to 2
- upper_inverse: bfloat16 [4, 16, 512, 8, 1024], P(None, None, 'col', None, 'row'), may hold values from -0.1 to 2
- right_side: float32 [32, 1024], P(None, 'row'), may hold values from -6 to 6
- first_guess: float32 [64, 512], P(None, 'col'), may hold values from -6 to 6
Outputs:
- solution: float32 [64, 512], P(None, 'col')
- hessenberg: float32 [4, 3], replicated
All inputs are finite; a program needn't handle non-finite values.
Results may differ from a plain program's by a relative error of at most 0.011.
Values may be sent and summed in bfloat16 or wider, within the bound.
No kernel may reach another device: no remote copies, remote signals or barrier semaphores. Data moves between devices by JAX's collectives and lax.ppermute only.
A program may use at most 320 MiB of HBM per device.

v0:
```python
import jax
import jax.numpy as jnp
from jax import lax
from jax.sharding import PartitionSpec as P

ORDER = 32768
SWEEPS = 4
ITERS = 3
DIAG_ORDER = 8192
DIAG_SHIFT = 2.0


def scrambled(tile_seed, flat_index):
    hashed = tile_seed + flat_index * 1640531527
    hashed = hashed ^ hashed >> 16 & 65535
    hashed = hashed * 2146121005
    hashed = hashed ^ hashed >> 15 & 131071
    hashed = hashed * 1779033703
    hashed = hashed ^ hashed >> 16 & 65535
    high_bits = hashed >> 8 & 16777215
    return (high_bits.astype(jnp.float32) - 8388607.5) / 8388608.0


def small_solve(normal_matrix, target):
    factor = jnp.linalg.cholesky(normal_matrix)
    order_small = normal_matrix.shape[0]
    forward = []
    for position in range(order_small):
        partial_value = target[position]
        for earlier in range(position):
            partial_value = partial_value - factor[position, earlier] * forward[earlier]
        forward.append(partial_value / factor[position, position])
    backward = [None] * order_small
    for position in reversed(range(order_small)):
        partial_value = forward[position]
        for after_pos in range(position + 1, order_small):
            partial_value = partial_value - factor[after_pos, position] * backward[after_pos]
        backward[position] = partial_value / factor[position, position]
    return backward


def matrix_part(seed_grid, vector_col, row_index, col_index, n_row, n_col):
    tile_size = vector_col.shape[1]
    offsets = jnp.arange(tile_size, dtype=jnp.int32)
    flat_index = offsets[:, None] * tile_size + offsets[None, :]
    col_tiles = jnp.arange(seed_grid.shape[1], dtype=jnp.int32)
    col_ids = (col_tiles[:, None] * n_col + col_index) * tile_size + offsets[None, :]
    entry_scale = ORDER ** (-0.5)

    def one_row(inputs):
        seed_row, tile_row = inputs
        values = scrambled(seed_row[None, :, None], flat_index[:, None, :]) * entry_scale
        row_ids = (tile_row * n_row + row_index) * tile_size + offsets
        values = values + jnp.where(row_ids[:, None, None] == col_ids[None, :, :], DIAG_SHIFT, 0.0)
        return jnp.einsum("icj,cj->i", values, vector_col, precision=lax.Precision.HIGHEST)

    return lax.map(one_row, (seed_grid, jnp.arange(seed_grid.shape[0], dtype=jnp.int32)))


def lower_sweep(vector_row, factors, lower_inverse, row_span, col_span):
    solved = []
    for sweep_step in range(SWEEPS):
        first_row = sweep_step * row_span
        target = vector_row[first_row : first_row + row_span]
        if sweep_step > 0:
            earlier = jnp.concatenate(solved, axis=0).astype(jnp.bfloat16)
            coupled = jnp.einsum(
                "minj,nj->mi",
                factors[first_row : first_row + row_span, :, : sweep_step * col_span, :],
                earlier,
                preferred_element_type=jnp.float32,
            )
            target = target - lax.psum(coupled, "col")
        mapped = jnp.einsum(
            "cimj,mj->ci",
            lower_inverse[sweep_step],
            target.astype(jnp.bfloat16),
            preferred_element_type=jnp.float32,
        )
        solved.append(lax.psum(mapped, "row"))
    return jnp.concatenate(solved, axis=0)


def upper_sweep(own_rows, factors, upper_inverse, row_span, col_span):
    solved = [None] * SWEEPS
    for sweep_step in reversed(range(SWEEPS)):
        first_row = sweep_step * row_span
        next_col = (sweep_step + 1) * col_span
        own_part = own_rows[first_row : first_row + row_span]
        if sweep_step < SWEEPS - 1:
            later_part = jnp.concatenate(solved[sweep_step + 1 :], axis=0).astype(jnp.bfloat16)
            coupled = jnp.einsum(
                "minj,nj->mi",
                factors[first_row : first_row + row_span, :, next_col:, :],
                later_part,
                preferred_element_type=jnp.float32,
            )
            sent = -coupled
            target = (own_part + lax.psum(sent, "col")).astype(jnp.bfloat16)
        else:
            target = own_part.astype(jnp.bfloat16)
        mapped = jnp.einsum(
            "cimj,mj->ci", upper_inverse[sweep_step], target, preferred_element_type=jnp.float32
        )
        solved[sweep_step] = lax.psum(mapped, "row")
    return jnp.concatenate(solved, axis=0)


def shards(tile_seeds, factors, lower_inverse, upper_inverse, right_side, first_guess):
    n_row = lax.axis_size("row")
    n_col = lax.axis_size("col")
    row_index = lax.axis_index("row")
    col_index = lax.axis_index("col")
    seed_grid = tile_seeds[:, 0, :, 0]
    tile_size = right_side.shape[1]
    row_span = DIAG_ORDER // (tile_size * n_row)
    col_span = DIAG_ORDER // (tile_size * n_col)

    def apply_system(vector_col):
        partial_value = matrix_part(seed_grid, vector_col, row_index, col_index, n_row, n_col)
        return lax.psum(partial_value, "col")

    residual = right_side - apply_system(first_guess)
    initial_norm = jnp.sqrt(lax.psum(jnp.sum(residual * residual), "row"))
    basis_list = [residual / initial_norm]
    directions = []
    hessenberg = jnp.zeros((ITERS + 1, ITERS), jnp.float32)
    for column in range(ITERS):
        lowered = lower_sweep(basis_list[column], factors, lower_inverse, row_span, col_span)
        gathered = lax.all_gather(lowered, "col", axis=1, tiled=True)
        spread = gathered.reshape(-1, n_row, tile_size)
        own_rows = lax.dynamic_index_in_dim(spread, row_index, 1, keepdims=False)
        direction = upper_sweep(own_rows, factors, upper_inverse, row_span, col_span)
        directions.append(direction)
        mapped = apply_system(direction)
        stacked = jnp.stack(basis_list)
        coeffs, squared = lax.psum(
            (jnp.sum(stacked * mapped[None], axis=(1, 2)), jnp.sum(mapped * mapped)), "row"
        )
        mapped = mapped - jnp.sum(coeffs[:, None, None] * stacked, axis=0)
        length = jnp.sqrt(squared - jnp.sum(coeffs * coeffs))
        hessenberg = (
            hessenberg.at[: column + 1, column].set(coeffs).at[column + 1, column].set(length)
        )
        if column + 1 < ITERS:
            basis_list.append(mapped / length)
    normal_matrix = jnp.dot(hessenberg.T, hessenberg, precision=lax.Precision.HIGHEST)
    weights = small_solve(normal_matrix, initial_norm * hessenberg[0])
    solution = first_guess
    for position in range(ITERS):
        solution = solution + weights[position] * directions[position]
    return (solution, hessenberg)


def solution(mesh):
    in_specs = (
        P(None, "row", None, "col"),
        P(None, "row", None, "col"),
        P(None, None, "col", None, "row"),
        P(None, None, "col", None, "row"),
        P(None, "row"),
        P(None, "col"),
    )
    out_specs = (P(None, "col"), P())
    return jax.shard_map(shards, mesh=mesh, in_specs=in_specs, out_specs=out_specs, check_vma=False)
```

profile of v0, /device:TPU:0, one launch (start us, length us, event | category | flops | bytes accessed | tf_op | source)
XLA Modules:
  0.0 2343.3 jit_solution(12727246034049527136)
XLA Ops:
  0.7 321.6 %while.58 = (s32[]{:T(128)}, f32[32,128]{1,0:T(8,128)S(1)}, s32[32,64]{1,0:T(8,128)}, s32[32]{0:T(128)S(1)}, s32[]{:T(128)}, /*index=5*/f32[64,128]{1,0:T(8,128)...) while((s32[]{:T(128)}, f32[32,128]{1,0:T(8,128)S(1)}, ...), condition=%wide.region_1.2_spmd.clone, body=%wide.region_0.1_spmd.clone.sunk | while | flops 33595524 | bytes 8753357 | solution.py:57
  335.6 22.3 psum.372
  380.6 17.4 psum.373
  413.9 17.8 psum.374
  441.4 19.4 psum.375
  506.1 17.4 psum.377
  523.5 18.5 fusion.192
  542.0 17.7 copy.38
  580.5 19.4 psum.379
  669.6 19.4 psum.382
  721.7 17.4 psum.384
  739.1 17.7 copy.59
  777.8 19.8 psum.386
  797.6 316.5 %while.59 = (s32[]{:T(128)}, f32[32,128]{1,0:T(8,128)S(1)}, s32[32,64]{1,0:T(8,128)}, s32[32]{0:T(128)S(1)}, s32[]{:T(128)}, /*index=5*/f32[64,128]{1,0:T(8,128)...) while((s32[]{:T(128)}, f32[32,128]{1,0:T(8,128)S(1)}, ...), condition=%wide.region_20.21_spmd.clone, body=%wide.region_19.20_spmd.clone.sunk | while | flops 33595524 | bytes 8622257 | solution.py:57
  1124.8 17.8 all-reduce.3
  1148.0 19.4 psum.390
  1209.4 19.5 psum.394
  1268.8 19.4 psum.397
  1330.3 19.4 psum.401
  1363.9 17.6 psum.403
  1381.5 317.2 %while.60 = (s32[]{:T(128)}, f32[32,128]{1,0:T(8,128)S(1)}, s32[32,64]{1,0:T(8,128)}, s32[32]{0:T(128)S(1)}, s32[]{:T(128)}, /*index=5*/f32[64,128]{1,0:T(8,128)...) while((s32[]{:T(128)}, f32[32,128]{1,0:T(8,128)S(1)}, ...), condition=%wide.region_42.43_spmd.clone, body=%wide.region_41.42_spmd.clone.sunk | while | flops 33595524 | bytes 8622257 | solution.py:57
  1709.5 19.8 all-reduce.2
  1734.2 17.4 psum.407
  1763.0 19.3 psum.409
  1795.5 17.8 psum.411
  1827.6 19.3 psum.413
  1855.2 17.4 psum.414
  1884.1 19.3 psum.416
  1916.6 17.4 psum.418
  1948.2 19.5 psum.420
  1967.8 320.8 %while.61 = (s32[]{:T(128)}, f32[32,128]{1,0:T(8,128)S(1)}, s32[32,64]{1,0:T(8,128)}, s32[32]{0:T(128)S(1)}, s32[]{:T(128)}, /*index=5*/f32[64,128]{1,0:T(8,128)...) while((s32[]{:T(128)}, f32[32,128]{1,0:T(8,128)S(1)}, ...), condition=%wide.region_66.67_spmd.clone, body=%wide.region_65.66_spmd.clone.sunk | while | flops 33595524 | bytes 8622257 | solution.py:57
  2299.4 17.8 all-reduce.1
  (1316 shorter events, 1712.6 us)
Async XLA Ops:
  0.7 334.3 %copy-start.2 = (f32[32,128]{1,0:T(8,128)S(1)}, f32[32,128]{1,0:T(8,128)}, u32[]{:S(2)}) copy-start(f32[32,128]{1,0:T(8,128)} %param.30) | copy-start | bytes 49156
  0.7 4.7 copy-start
  10.8 4.7 copy-start
  20.8 4.7 copy-start
  30.9 4.7 copy-start
  40.9 4.7 copy-start
  50.9 4.7 copy-start
  61.0 4.7 copy-start
  71.0 4.7 copy-start
  81.1 4.7 copy-start
  91.1 4.7 copy-start
  101.2 4.7 copy-start
  111.2 4.7 copy-start
  121.3 4.7 copy-start
  131.3 4.7 copy-start
  141.4 4.7 copy-start
  151.4 4.7 copy-start
  161.5 4.7 copy-start
  171.5 4.7 copy-start
  181.6 4.7 copy-start
  191.6 4.7 copy-start
  201.7 4.7 copy-start
  211.7 4.7 copy-start
  221.8 4.7 copy-start
  231.8 4.7 copy-start
  241.9 4.7 copy-start
  262.0 4.7 copy-start
  272.0 4.7 copy-start
  292.1 4.7 copy-start
  302.2 4.7 copy-start
  1967.8 357.4 %copy-start.3 = (s32[2]{0:T(128)S(1)}, s32[2]{0:T(128)}, u32[]{:S(2)}) copy-start(s32[2]{0:T(128)} %constant.590.clone.1) | copy-start | bytes 28
  1967.8 374.0 %copy-start.1 = (f32[64,128]{1,0:T(8,128)S(1)}, f32[64,128]{1,0:T(8,128)}, u32[]{:S(2)}) copy-start(f32[64,128]{1,0:T(8,128)} %get-tuple-element.1081) | copy-start | bytes 98308
  (3 other events, 14.0 us)
where the time goes:
time: 2360 us; the launch traced here: 2340 us
  matrix products  827 us (35%)
  blocking collectives  695 us (29%)
  local copies, waits for them, and re-layouts  372 us (16%)
  other arithmetic  341 us (14%)
  loops' own time  92.1 us (4%)
    dot_general x128, matrix products, one_row(): jnp.einsum('icj,cj->i', values, vector_col, precision=lax.Precision.HIGHEST)  681 us
    add x128, other arithmetic, one_row(): values + jnp.where(row_ids[:, None, None] == col_ids[None, :, :], DIAG_SH...  309 us
    psum x12, blocking collectives, upper_sweep(): solved[sweep_step] = lax.psum(mapped, 'row')  221 us
    psum x12, blocking collectives, lower_sweep(): solved.append(lax.psum(mapped, 'row'))  221 us
    another operation x4, loops' own time, matrix_part(): lax.map(one_row, (seed_grid, jnp.arange(seed_grid.shape[0], dtype=jnp.int...  92.1 us
    add x128, local copies, waits for them, and re-layouts, scrambled(): hashed = tile_seed + flat_index * 1640531527  89.3 us
    dynamic_slice x128, local copies, waits for them, and re-layouts, matrix_part(): lax.map(one_row, (seed_grid, jnp.arange(seed_grid.shape[0], dtype=jnp.int...  81.4 us
    slice x6, local copies, waits for them, and re-layouts, upper_sweep(): factors[first_row:first_row + row_span, :, next_col:, :]  74.7 us

commit v1 on v0

--- a/solution.py
+++ b/solution.py
@@ -2,6 +2,7 @@
 import jax.numpy as jnp
 from jax import lax
 from jax.sharding import PartitionSpec as P
+from jax.lax import all_gather
 
 ORDER = 32768
 SWEEPS = 4
@@ -102,7 +103,7 @@
         mapped = jnp.einsum(
             "cimj,mj->ci", upper_inverse[sweep_step], target, preferred_element_type=jnp.float32
         )
-        solved[sweep_step] = lax.psum(mapped, "row")
+        solved[sweep_step] = jnp.sum(all_gather(mapped, axis_name="row"), axis=0)
     return jnp.concatenate(solved, axis=0)
 
 

time: 2360 us -> 2480 us (1.051)
  blocking collectives: 695 us -> 829 us
    all_gather x0 -> x12, blocking collectives: none -> 367 us  [upper_sweep(): solved[sweep_step] = jnp.sum(all_gather(mapped, axis_name='row'), axis=0)]
    psum x12 -> x0, blocking collectives: 221 us -> none  [upper_sweep(): solved[sweep_step] = lax.psum(mapped, 'row')]
where the time goes in v1:
time: 2480 us; the launch traced here: 2470 us
  blocking collectives  829 us (33%)
  matrix products  827 us (33%)
  local copies, waits for them, and re-layouts  367 us (15%)
  other arithmetic  341 us (14%)
  loops' own time  84.9 us (3%)
    dot_general x128, matrix products, one_row(): jnp.einsum('icj,cj->i', values, vector_col, precision=lax.Precision.HIGHEST)  681 us
    all_gather x12, blocking collectives, upper_sweep(): solved[sweep_step] = jnp.sum(all_gather(mapped, axis_name='row'), axis=0)  367 us
    add x128, other arithmetic, one_row(): values + jnp.where(row_ids[:, None, None] == col_ids[None, :, :], DIAG_SH...  309 us
    psum x12, blocking collectives, lower_sweep(): solved.append(lax.psum(mapped, 'row'))  221 us
    add x128, local copies, waits for them, and re-layouts, scrambled(): hashed = tile_seed + flat_index * 1640531527  89.3 us
    another operation x4, loops' own time, matrix_part(): lax.map(one_row, (seed_grid, jnp.arange(seed_grid.shape[0], dtype=jnp.int...  84.9 us
    dynamic_slice x128, local copies, waits for them, and re-layouts, matrix_part(): lax.map(one_row, (seed_grid, jnp.arange(seed_grid.shape[0], dtype=jnp.int...  76.8 us
    slice x6, local copies, waits for them, and re-layouts, upper_sweep(): factors[first_row:first_row + row_span, :, next_col:, :]  74.7 us

profile of v1, /device:TPU:0, one launch (start us, length us, event | category | flops | bytes accessed | tf_op | source)
XLA Modules:
  0.0 2465.3 jit_solution(8285756175983078)
XLA Ops:
  0.7 321.6 %while.58 = (s32[]{:T(128)}, f32[32,128]{1,0:T(8,128)S(1)}, s32[32,64]{1,0:T(8,128)}, s32[32]{0:T(128)S(1)}, s32[]{:T(128)}, /*index=5*/f32[64,128]{1,0:T(8,128)...) while((s32[]{:T(128)}, f32[32,128]{1,0:T(8,128)S(1)}, ...), condition=%wide.region_1.2_spmd.clone, body=%wide.region_0.1_spmd.clone.sunk | while | flops 33595524 | bytes 8753357 | solution.py:58
  335.6 22.3 psum.288
  429.4 19.4 psum.291
  511.6 18.5 fusion.190
  530.0 17.7 copy.40
  568.7 19.4 psum.295
  615.3 30.5 %all-gather = f32[128,128]{1,0:T(8,128)S(1)} all-gather(f32[16,128]{1,0:T(8,128)S(1)} %bitcast.441), channel_id=2, replica_groups=mesh['row'=8,'col'=4] {'row'}, dimensions={0}, use_global_device_ids=true | all-gather | bytes 73728 | tf_op jit(solution)/shard_map/all_gather | solution.py:106
  670.9 30.5 %all-gather.1 = f32[128,128]{1,0:T(8,128)S(1)} all-gather(f32[16,128]{1,0:T(8,128)S(1)} %bitcast.435), channel_id=3, replica_groups=mesh['row'=8,'col'=4] {'row'}, dimensions={0}, use_global_device_ids=true | all-gather | bytes 73728 | tf_op jit(solution)/shard_map/all_gather | solution.py:106
  734.3 30.5 %all-gather.2 = f32[128,128]{1,0:T(8,128)S(1)} all-gather(f32[16,128]{1,0:T(8,128)S(1)} %bitcast.436), channel_id=4, replica_groups=mesh['row'=8,'col'=4] {'row'}, dimensions={0}, use_global_device_ids=true | all-gather | bytes 73728 | tf_op jit(solution)/shard_map/all_gather | solution.py:106
  764.8 17.7 copy.61
  803.4 30.9 %all-gather.3 = f32[128,128]{1,0:T(8,128)S(1)} all-gather(f32[16,128]{1,0:T(8,128)S(1)} %bitcast.437), channel_id=5, replica_groups=mesh['row'=8,'col'=4] {'row'}, dimensions={0}, use_global_device_ids=true | all-gather | bytes 73728 | tf_op jit(solution)/shard_map/all_gather | solution.py:106
  834.4 312.8 %while.59 = (s32[]{:T(128)}, f32[32,128]{1,0:T(8,128)S(1)}, s32[32,64]{1,0:T(8,128)}, s32[32]{0:T(128)S(1)}, s32[]{:T(128)}, /*index=5*/f32[64,128]{1,0:T(8,128)...) while((s32[]{:T(128)}, f32[32,128]{1,0:T(8,128)S(1)}, ...), condition=%wide.region_20.21_spmd.clone, body=%wide.region_19.20_spmd.clone.sunk | while | flops 33595524 | bytes 8622257 | solution.py:58
  1157.9 17.8 all-reduce.3
  1180.9 19.4 psum.302
  1242.3 19.5 psum.306
  1276.1 17.4 psum.308
  1301.7 30.5 %all-gather.4 = f32[128,128]{1,0:T(8,128)S(1)} all-gather(f32[16,128]{1,0:T(8,128)S(1)} %bitcast.442), channel_id=6, replica_groups=mesh['row'=8,'col'=4] {'row'}, dimensions={0}, use_global_device_ids=true | all-gather | bytes 73728 | tf_op jit(solution)/shard_map/all_gather | solution.py:106
  1343.8 30.5 %all-gather.5 = f32[128,128]{1,0:T(8,128)S(1)} all-gather(f32[16,128]{1,0:T(8,128)S(1)} %bitcast.438), channel_id=7, replica_groups=mesh['row'=8,'col'=4] {'row'}, dimensions={0}, use_global_device_ids=true | all-gather | bytes 73728 | tf_op jit(solution)/shard_map/all_gather | solution.py:106
  1387.5 30.5 %all-gather.6 = f32[128,128]{1,0:T(8,128)S(1)} all-gather(f32[16,128]{1,0:T(8,128)S(1)} %bitcast.439), channel_id=8, replica_groups=mesh['row'=8,'col'=4] {'row'}, dimensions={0}, use_global_device_ids=true | all-gather | bytes 73728 | tf_op jit(solution)/shard_map/all_gather | solution.py:106
  1432.3 30.7 %all-gather.7 = f32[128,128]{1,0:T(8,128)S(1)} all-gather(f32[16,128]{1,0:T(8,128)S(1)} %bitcast.440), channel_id=9, replica_groups=mesh['row'=8,'col'=4] {'row'}, dimensions={0}, use_global_device_ids=true | all-gather | bytes 73728 | tf_op jit(solution)/shard_map/all_gather | solution.py:106
  1463.1 316.0 %while.60 = (s32[]{:T(128)}, f32[32,128]{1,0:T(8,128)S(1)}, s32[32,64]{1,0:T(8,128)}, s32[32]{0:T(128)S(1)}, s32[]{:T(128)}, /*index=5*/f32[64,128]{1,0:T(8,128)...) while((s32[]{:T(128)}, f32[32,128]{1,0:T(8,128)S(1)}, ...), condition=%wide.region_42.43_spmd.clone, body=%wide.region_41.42_spmd.clone.sunk | while | flops 33595524 | bytes 8622257 | solution.py:58
  1789.9 19.7 all-reduce.2
  1814.4 17.4 psum.315
  1843.3 19.3 psum.317
  1875.8 17.8 psum.319
  1907.8 19.3 psum.321
  1935.4 30.5 %all-gather.8 = f32[128,128]{1,0:T(8,128)S(1)} all-gather(f32[16,128]{1,0:T(8,128)S(1)} %bitcast.431), channel_id=10, replica_groups=mesh['row'=8,'col'=4] {'row'}, dimensions={0}, use_global_device_ids=true | all-gather | bytes 73728 | tf_op jit(solution)/shard_map/all_gather | solution.py:106
  1977.4 30.5 %all-gather.9 = f32[128,128]{1,0:T(8,128)S(1)} all-gather(f32[16,128]{1,0:T(8,128)S(1)} %bitcast.432), channel_id=11, replica_groups=mesh['row'=8,'col'=4] {'row'}, dimensions={0}, use_global_device_ids=true | all-gather | bytes 73728 | tf_op jit(solution)/shard_map/all_gather | solution.py:106
  2021.2 30.5 %all-gather.10 = f32[128,128]{1,0:T(8,128)S(1)} all-gather(f32[16,128]{1,0:T(8,128)S(1)} %bitcast.433), channel_id=12, replica_groups=mesh['row'=8,'col'=4] {'row'}, dimensions={0}, use_global_device_ids=true | all-gather | bytes 73728 | tf_op jit(solution)/shard_map/all_gather | solution.py:106
  2066.0 30.7 %all-gather.11 = f32[128,128]{1,0:T(8,128)S(1)} all-gather(f32[16,128]{1,0:T(8,128)S(1)} %bitcast.434), channel_id=13, replica_groups=mesh['row'=8,'col'=4] {'row'}, dimensions={0}, use_global_device_ids=true | all-gather | bytes 73728 | tf_op jit(solution)/shard_map/all_gather | solution.py:106
  2096.7 313.8 %while.61 = (s32[]{:T(128)}, f32[32,128]{1,0:T(8,128)S(1)}, s32[32,64]{1,0:T(8,128)}, s32[32]{0:T(128)S(1)}, s32[]{:T(128)}, /*index=5*/f32[64,128]{1,0:T(8,128)...) while((s32[]{:T(128)}, f32[32,128]{1,0:T(8,128)S(1)}, ...), condition=%wide.region_66.67_spmd.clone, body=%wide.region_65.66_spmd.clone.sunk | while | flops 33595524 | bytes 8622257 | solution.py:58
  2421.4 17.8 all-reduce.1
  (1319 shorter events, 1696.5 us)
Async XLA Ops:
  0.7 334.3 %copy-start.2 = (f32[32,128]{1,0:T(8,128)S(1)}, f32[32,128]{1,0:T(8,128)}, u32[]{:S(2)}) copy-start(f32[32,128]{1,0:T(8,128)} %param.30) | copy-start | bytes 49156
  0.7 4.7 copy-start
  10.8 4.7 copy-start
  20.8 4.7 copy-start
  30.9 4.7 copy-start
  40.9 4.7 copy-start
  50.9 4.7 copy-start
  61.0 4.7 copy-start
  71.0 4.7 copy-start
  81.1 4.7 copy-start
  91.1 4.7 copy-start
  101.2 4.7 copy-start
  111.2 4.7 copy-start
  121.3 4.7 copy-start
  131.3 4.7 copy-start
  141.4 4.7 copy-start
  151.4 4.7 copy-start
  161.5 4.7 copy-start
  171.5 4.7 copy-start
  181.6 4.7 copy-start
  191.6 4.7 copy-start
  201.7 4.7 copy-start
  211.7 4.7 copy-start
  221.8 4.7 copy-start
  231.8 4.7 copy-start
  251.9 4.7 copy-start
  262.0 4.7 copy-start
  282.1 4.7 copy-start
  292.1 4.7 copy-start
  312.2 4.7 copy-start
  2096.7 350.5 %copy-start.3 = (s32[2]{0:T(128)S(1)}, s32[2]{0:T(128)}, u32[]{:S(2)}) copy-start(s32[2]{0:T(128)} %constant.590.clone.1) | copy-start | bytes 28
  2096.7 367.1 %copy-start.1 = (f32[64,128]{1,0:T(8,128)S(1)}, f32[64,128]{1,0:T(8,128)}, u32[]{:S(2)}) copy-start(f32[64,128]{1,0:T(8,128)} %get-tuple-element.1080) | copy-start | bytes 98308
  (3 other events, 14.0 us)
